TPU v7x, 256 devices: a whole 4x4x8 slice. The times are simulated.
256 devices in a mesh: grp: 4 (over y), dev: 64 (over z, x, core).
Axes of the slice: x: 4, y: 4, z: 8, core: 2. Of those that a mesh axis runs over, the one named last changes fastest.
Arguments:
- nz_user: int32 [32768, 128], P(('grp', 'dev')), may hold values from 0 to 65535
- nz_sub: int32 [32768, 128], P(('grp', 'dev')), may hold values from 0 to 16383
- nz_value: float32 [32768, 128], P(('grp', 'dev')), may hold values from -1 to 1
- tile_word: int32 [32768], P(('grp', 'dev')), may hold values from 0 to 16383, as said below
- word_owner: int32 [16384], replicated, may hold values from 0 to 16383, as said below
- user_factor: bfloat16 [64, 65536], P(None, 'dev'), may hold values from -6 to 6
- sub_factor: bfloat16 [64, 16384], P(None, 'dev'), may hold values from -6 to 6
Outputs:
- word_rows: float32 [64, 16384], P(None, ('grp', 'dev'))
Inputs may be any that keep to these rules, and one draw needn't show every extreme that they name: A permutation of the word indices: word w is summed into column word_owner[w] of word_rows. `tile_word`: tile i lies on device i // 128 (grp+dev order). On every device at most 2 tiles belong to words whose output column lies on any one other device, and on every device that bound is reached for some other device.
All inputs are finite; a program needn't handle non-finite values.
Results may differ from a plain program's by a relative error of at most 0.0003.
Values may be sent and summed in bfloat16 or wider, within the bound.
A program may use at most 64 MiB of HBM per device.

v0:
```python
import jax
import jax.numpy as jnp
from jax import lax
from jax.sharding import PartitionSpec as P

CAP = 2


def cut_along(value, dim, peers):
    shape = value.shape
    pieces = value.reshape(*shape[:dim], peers, shape[dim] // peers, *shape[dim + 1 :])
    return jnp.moveaxis(pieces, dim, 0)


def joined_along(pieces, dim):
    pieces = jnp.moveaxis(pieces, 0, dim)
    shape = pieces.shape
    return pieces.reshape(*shape[:dim], shape[dim] * shape[dim + 1], *shape[dim + 2 :])


def exchange_both(value, axis, axes, splits, concats):
    sizes = [lax.axis_size(a) for a in axes]
    pieces = cut_along(value, splits[0], sizes[0])
    pieces = jnp.moveaxis(cut_along(pieces, splits[1] + 1, sizes[1]), 0, 1)
    inside = pieces.shape[2:]
    pieces = pieces.reshape(-1, *inside)
    pieces = lax.all_to_all(pieces, axis, split_axis=0, concat_axis=0, tiled=True)
    pieces = joined_along(pieces.reshape(*sizes, *inside), concats[0] + 1)
    return joined_along(pieces, concats[1])


def tile_sums(user_table, sub_table, nz_user, nz_sub, nz_value):
    tile_count, tile_width = nz_user.shape
    block_tiles = min(tile_count, 128)
    block_count = tile_count // block_tiles

    def one_block(block_args):
        users_block, subs_block, vals_block = block_args
        user_rows = jnp.take(user_table, users_block, axis=0).astype(jnp.float32)
        sub_rows = jnp.take(sub_table, subs_block, axis=0).astype(jnp.float32)
        return jnp.sum(user_rows * sub_rows * vals_block[:, :, None], axis=1)

    block_sums = lax.map(
        one_block,
        (
            nz_user.reshape(block_count, block_tiles, tile_width),
            nz_sub.reshape(block_count, block_tiles, tile_width),
            nz_value.reshape(block_count, block_tiles, tile_width),
        ),
    )
    return block_sums.reshape(tile_count, block_sums.shape[2])


def shards(nz_user, nz_sub, nz_value, tile_word, word_owner, user_factor, sub_factor):
    users_all, subs_all = (
        lax.all_gather(user_factor, "dev", axis=1, tiled=True),
        lax.all_gather(sub_factor, "dev", axis=1, tiled=True),
    )
    user_table = jnp.transpose(users_all)
    sub_table = jnp.transpose(subs_all)
    tile_rows = tile_sums(user_table, sub_table, nz_user, nz_sub, nz_value)
    tile_count, rank_width = tile_rows.shape
    grp_size = lax.axis_size("grp")
    dev_size = lax.axis_size("dev")
    devices_all = grp_size * dev_size
    words_total = word_owner.shape[0]
    words_local = words_total // devices_all
    out_rows = jnp.take(word_owner, tile_word)
    self_index = lax.axis_index("grp") * dev_size + lax.axis_index("dev")
    owner_dev = out_rows // words_local
    local_row = out_rows - owner_dev * words_local
    owned = owner_dev == self_index
    columns = jnp.arange(words_local, dtype=jnp.int32)
    own_table = (owned[:, None] & (local_row[:, None] == columns[None, :])).astype(jnp.float32)
    own_part = jnp.einsum("tr,tk->rk", tile_rows, own_table, precision=lax.Precision.HIGHEST)
    peer_ids = jnp.arange(devices_all, dtype=jnp.int32)
    outgoing = (jnp.logical_not(owned)[:, None] & (owner_dev[:, None] == peer_ids[None, :])).astype(
        jnp.float32
    )
    tile_ids = jnp.arange(tile_count, dtype=jnp.int32)
    earlier_table = (tile_ids[:, None] > tile_ids[None, :]).astype(jnp.float32)
    earlier = jnp.dot(
        earlier_table, outgoing, precision=lax.Precision.HIGHEST, preferred_element_type=jnp.float32
    )
    position = jnp.sum(earlier * outgoing, axis=1).astype(jnp.int32)
    send_slot = jnp.where(owned, devices_all * CAP, owner_dev * CAP + position)
    slot_ids = jnp.arange(devices_all * CAP, dtype=jnp.int32)
    slot_table = (send_slot[:, None] == slot_ids[None, :]).astype(jnp.float32)
    send_rows = jnp.einsum("ts,tr->sr", slot_table, tile_rows, precision=lax.Precision.HIGHEST)
    filled = jnp.sum(slot_table, axis=0)
    send_ids = (
        jnp.dot(
            local_row.astype(jnp.float32),
            slot_table,
            precision=lax.Precision.HIGHEST,
            preferred_element_type=jnp.float32,
        )
        + filled
        - 1.0
    )
    send_rows = send_rows.reshape(grp_size, dev_size, CAP * rank_width)
    send_ids = send_ids.reshape(grp_size, dev_size, CAP)
    got_rows, got_ids = (
        exchange_both(send_rows, ("dev", "grp"), ("dev", "grp"), (1, 0), (1, 0)),
        exchange_both(send_ids, ("dev", "grp"), ("dev", "grp"), (1, 0), (1, 0)),
    )
    got_rows = got_rows.reshape(devices_all * CAP, rank_width)
    got_ids = got_ids.reshape(devices_all * CAP).astype(jnp.int32)
    got_table = (got_ids[:, None] == columns[None, :]).astype(jnp.float32)
    far_part = jnp.einsum("sr,sk->rk", got_rows, got_table, precision=lax.Precision.HIGHEST)
    return own_part + far_part


def solution(mesh):
    return jax.shard_map(
        shards,
        mesh=mesh,
        in_specs=(
            P(("grp", "dev"), None),
            P(("grp", "dev"), None),
            P(("grp", "dev"), None),
            P(("grp", "dev")),
            P(),
            P(None, "dev"),
            P(None, "dev"),
        ),
        out_specs=P(None, ("grp", "dev")),
        check_vma=False,
    )
```

profile of v0, /device:TPU:1, one launch (start us, length us, event | category | flops | bytes accessed | tf_op | source)
XLA Modules:
  0.0 297.3 jit_solution(12197286190946821888)
XLA Ops:
  6.5 1.5 copy.45
  8.1 1.8 copy.44
  9.9 0.7 compare_select_fusion.2
  10.6 1.1 gather_fusion.2
  11.8 0.7 fusion.17
  12.4 0.3 fusion
  12.8 0.7 add_select_fusion
  13.4 0.1 convert_reduce_fusion
  13.6 0.3 fusion.1
  13.8 0.1 reshape_reshape.14
  14.0 0.7 copy.55
  14.7 15.6 %all-to-all-start.1 = ((f32[256,1,1,2]{3,2,1,0:T(1,128)}), f32[256,1,1,2]{3,2,1,0:T(1,128)S(1)}, u32[]{:S(2)}, u32[]{:S(2)}) async-start(f32[256,1,1,2]{3,2,1,0:T(1,128)} %bitcast.14), calls=%async_computation.1 | async-start | bytes 262144 | tf_op jit(solution)/shard_map/all_to_all | solution.py:27
  30.4 0.9 compare_and_fusion
  31.3 0.9 bitcast_clamp_fusion.1
  32.1 0.9 bitcast_clamp_fusion
  33.0 60.6 %all-gather.5.cloned.1.call-done = bf16[64,16384]{0,1:T(8,128)(2,1)} async-done(((bf16[64,256]{0,1:T(8,128)(2,1)}), bf16[64,16384]{0,1:T(8,128)(2,1)}) %all-gather.5.cloned.1.call-update) | async-done | bytes 2097168 | tf_op jit(solution)/shard_map/all_gather | solution.py:57
  93.6 58.1 %gather_fusion.1 = bf16[16384,64]{1,0:T(8,128)(2,1)} fusion(bf16[16384,64]{1,0:T(8,128)(2,1)} %bitcast.38, s32[16384]{0:T(1024)S(1)} %bitcast_clamp_fusion), kind=kCustom, calls=%fused_computation.1 | custom fusion | bytes 4259840 | tf_op jit(solution)/shard_map/while/body/eval_jaxpr/jit(_take)/gather | solution.py:40
  151.8 41.1 %all-gather.3.cloned.1.call-done = bf16[64,65536]{0,1:T(8,128)(2,1)} async-done(((bf16[64,1024]{0,1:T(8,128)(2,1)}), bf16[64,65536]{0,1:T(8,128)(2,1)}) %all-gather.3.cloned.1.call-update) | async-done | bytes 8388624 | tf_op jit(solution)/shard_map/all_gather | solution.py:56
  192.8 63.3 %gather_fusion = bf16[16384,64]{1,0:T(8,128)(2,1)} fusion(bf16[65536,64]{1,0:T(8,128)(2,1)} %bitcast.39, s32[16384]{0:T(1024)S(1)} %bitcast_clamp_fusion.1), kind=kCustom, calls=%fused_computation | custom fusion | bytes 4259840 | tf_op jit(solution)/shard_map/while/body/eval_jaxpr/jit(_take)/gather | solution.py:39
  256.2 10.6 %multiply_reduce_fusion = f32[128,64]{1,0:T(8,128)S(1)} fusion(f32[128,128]{1,0:T(8,128)S(1)} %copy-done.1, pred[128,128]{1,0:T(8,128)(4,1)S(1)} %get-tuple-element.30, pred[128,128]{1,0:T(8,128)(4,1)S(1)} %get-tuple-element.32, bf16[16384,64]{1,0:T(8,128)(2,1)} %gather_fusion.1, bf16[16384,64]{1,0:T(8,128)(2,1)} %gather_fusion), kind=kLoop, calls=%fused_computation.3 | loop fusion | flops 7331840 | bytes 4325376 | tf_op jit(solution)/shard_map/while/body/eval_jaxpr/reduce_sum | solution.py:41
  266.8 0.5 fusion.2
  267.2 0.1 reshape_reshape.12
  267.3 0.7 copy.47
  268.1 8.5 %all-to-all-start = ((f32[256,1,1,128]{3,2,1,0:T(1,128)}), f32[256,1,1,128]{3,2,1,0:T(1,128)S(1)}, u32[]{:S(2)}, u32[]{:S(2)}) async-start(f32[256,1,1,128]{3,2,1,0:T(1,128)} %bitcast.8), calls=%async_computation | async-start | bytes 262144 | tf_op jit(solution)/shard_map/all_to_all | solution.py:27
  276.6 0.1 copy.52
  276.6 0.1 convert_element_type.45
  276.8 0.6 copy.53
  277.3 0.2 convert_element_type.47
  277.5 0.3 fusion.11
  277.8 11.5 %all-to-all-done = f32[256,1,1,128]{3,2,1,0:T(1,128)S(1)} async-done(((f32[256,1,1,128]{3,2,1,0:T(1,128)}), f32[256,1,1,128]{3,2,1,0:T(1,128)S(1)}, u32[]{:S(2)}, u32[]{:S(2)}) %all-to-all-start) | async-done | bytes 131104 | tf_op jit(solution)/shard_map/all_to_all | solution.py:27
  289.3 0.1 reshape_reshape_reshape.4
  289.4 1.1 convolution_add_fusion
  (13 shorter events, 0.1 us)
Async XLA Ops:
  6.5 4.1 %copy-start = (s32[16384]{0:T(1024)S(1)}, s32[16384]{0:T(1024)}, u32[]{:S(2)}) copy-start(s32[16384]{0:T(1024)} %param.11) | copy-start | bytes 196612
  6.5 87.1 %all-gather.5.cloned.1.call-start = ((), (), s32[]{:S(2)}) async-start(), calls=%async_computation.3 | async-start | bytes 4259840 | tf_op jit(solution)/shard_map/all_gather | solution.py:57
  8.1 184.8 %all-gather.3.cloned.1.call-start = ((), (), s32[]{:S(2)}) async-start(), calls=%async_computation.2 | async-start | bytes 17039360 | tf_op jit(solution)/shard_map/all_gather | solution.py:56
  14.7 253.4 %all-to-all-start.1 = ((f32[256,1,1,2]{3,2,1,0:T(1,128)}), f32[256,1,1,2]{3,2,1,0:T(1,128)S(1)}, u32[]{:S(2)}, u32[]{:S(2)}) async-start(f32[256,1,1,2]{3,2,1,0:T(1,128)} %bitcast.14), calls=%async_computation.1 | async-start | bytes 262144 | tf_op jit(solution)/shard_map/all_to_all | solution.py:27
  192.8 63.3 %copy-start.1 = (f32[128,128]{1,0:T(8,128)S(1)}, f32[128,128]{1,0:T(8,128)}, u32[]{:S(2)}) copy-start(f32[128,128]{1,0:T(8,128)} %param.9) | copy-start | bytes 196612
  268.1 21.2 %all-to-all-start = ((f32[256,1,1,128]{3,2,1,0:T(1,128)}), f32[256,1,1,128]{3,2,1,0:T(1,128)S(1)}, u32[]{:S(2)}, u32[]{:S(2)}) async-start(f32[256,1,1,128]{3,2,1,0:T(1,128)} %bitcast.8), calls=%async_computation | async-start | bytes 262144 | tf_op jit(solution)/shard_map/all_to_all | solution.py:27
Sparse Core Ops, SparseCore 0:
  10.1 83.5 all-gather.4
  96.4 96.3 all-gather.2
where the time goes:
time: 298 us; the launch traced here: 297 us
  local copies, waits for them, and re-layouts  129 us (43%)
  waiting for transfers between devices  113 us (38%)
  starting transfers between devices  24.2 us (8%)
  other arithmetic  15.4 us (5%)
  between operations  13.5 us (5%)
    gather x1, local copies, waits for them, and re-layouts, one_block(): user_rows = jnp.take(user_table, users_block, axis=0).astype(jnp.float32)  63.3 us
    all_gather x1, waiting for transfers between devices, shards(): lax.all_gather(sub_factor, 'dev', axis=1, tiled=True)  60.6 us
    gather x1, local copies, waits for them, and re-layouts, one_block(): sub_rows = jnp.take(sub_table, subs_block, axis=0).astype(jnp.float32)  58.1 us
    all_gather x1, waiting for transfers between devices, shards(): lax.all_gather(user_factor, 'dev', axis=1, tiled=True)  41.1 us
    all_to_all x2, starting transfers between devices, exchange_both(): lax.all_to_all(pieces, axis, split_axis=0, concat_axis=0, tiled=True)  24.1 us
    all_to_all x2, waiting for transfers between devices, exchange_both(): lax.all_to_all(pieces, axis, split_axis=0, concat_axis=0, tiled=True)  11.5 us
    reduce_sum x1, other arithmetic, one_block(): return jnp.sum(user_rows * sub_rows * vals_block[:, :, None], axis=1)  10.6 us
  transfers between devices with their start and end apart: 4, of which 3 were waited for; matrix products, arithmetic and copies ran while one was open for 48% of the time, Pallas kernels for 0%

commit v1 on v0

--- a/solution.py
+++ b/solution.py
@@ -1,9 +1,326 @@
+import functools
+
 import jax
 import jax.numpy as jnp
 from jax import lax
+from jax.experimental import pallas as pl
+from jax.experimental.pallas import tpu as pltpu
 from jax.sharding import PartitionSpec as P
 
 CAP = 2
+MESH = pl.DeviceIdType.MESH
+NT, NZ, LANES = 128, 128, 128
+DEVS = 64
+U_ROWS, S_ROWS = 512, 128
+STEPS = 32
+TILES_STEP = NT // STEPS
+
+
+def kernel(
+    kc_ref, urow_ref, srow_ref, v0_ref, v1_ref, u_in, s_in, out_ref,
+    ub, sb, utab, stab, sv, g, kc_s, urow_s, srow_s,
+    send_u, send_s, recv_u, recv_s, loc,
+):
+    grp = lax.axis_index("grp")
+    dev = lax.axis_index("dev")
+    z, x, core = dev // 8, (dev // 2) % 4, dev % 2
+    partner = dev + 1 - 2 * core
+    lane = lax.broadcasted_iota(jnp.int32, (128, 128), 1)
+    sublane = lax.broadcasted_iota(jnp.int32, (128, 128), 0)
+
+    def at(dz, dx, c):
+        return ((z + dz + 8) % 8) * 8 + ((x + dx + 4) % 4) * 2 + c
+
+    local_copies = [
+        pltpu.make_async_copy(a, b, loc.at[i])
+        for i, (a, b) in enumerate(((kc_ref, kc_s), (srow_ref, srow_s), (urow_ref, urow_s)))
+    ]
+    for c in local_copies:
+        c.start()
+
+    barrier = pltpu.get_barrier_semaphore()
+    near = [
+        ((z + 1) % 8) * 8 + dev % 8,
+        ((z + 7) % 8) * 8 + dev % 8,
+        at(0, 1, core),
+        at(0, 3, core),
+        at(0, 2, core),
+        partner,
+    ]
+    for n in near:
+        pl.semaphore_signal(barrier, inc=1, device_id=(grp, n), device_id_type=MESH)
+    pl.semaphore_wait(barrier, len(near))
+
+    class Table:
+        def __init__(self, own, buf, rows, send, recv, convert):
+            self.own, self.buf, self.rows = own, buf, rows
+            self.send, self.recv, self.convert = send, recv, convert
+
+        def part(self, d, half):
+            rows = self.rows if half is None else self.rows // 2
+            first = d * self.rows + (0 if half is None else half * rows)
+            return self.buf.at[pl.ds(pl.multiple_of(first, 16), rows), :]
+
+        def put(self, d, to, half=None, own=False):
+            dst = self.part(d, half)
+            src = self.own if own else dst
+            pltpu.make_async_remote_copy(
+                src_ref=src, dst_ref=dst, send_sem=self.send,
+                recv_sem=self.recv.at[d, 0 if half is None else half],
+                device_id=(grp, to), device_id_type=MESH,
+            ).start()
+
+        def wait(self, d, half=None):
+            ref = self.part(d, half)
+            pltpu.make_async_remote_copy(
+                src_ref=ref, dst_ref=ref, send_sem=self.send,
+                recv_sem=self.recv.at[d, 0 if half is None else half],
+                device_id=(grp, partner), device_id_type=MESH,
+            ).wait_recv()
+
+        def sent(self):
+            ref = self.buf.at[pl.ds(0, 63 * self.rows), :]
+            pltpu.make_async_remote_copy(
+                src_ref=ref, dst_ref=ref, send_sem=self.send, recv_sem=self.recv.at[0, 0],
+                device_id=(grp, partner), device_id_type=MESH,
+            ).wait_send()
+
+        def take(self, d):
+            base = d * self.rows
+            self.convert(self.buf, base, base)
+
+    def convert_u(src, first, row):
+        @pl.loop(0, 4)
+        def _(i):
+            a = pl.multiple_of(first + i * 128, 128)
+            b = pl.multiple_of(row + i * 128, 128)
+            utab[pl.ds(b, 128), :] = src[pl.ds(a, 128), :].astype(jnp.float32)
+
+    def convert_s(src, first, row):
+        v = src[pl.ds(pl.multiple_of(first, 128), 128), :].astype(jnp.float32)
+        r = pltpu.roll(v, 64, 1)
+        stab[pl.ds(pl.multiple_of(2 * row, 128), 128), :] = jnp.where(lane < 64, v, r)
+        stab[pl.ds(pl.multiple_of(2 * row + 128, 128), 128), :] = jnp.where(lane < 64, r, v)
+
+    ut = Table(u_in, ub, U_ROWS, send_u, recv_u, convert_u)
+    st = Table(s_in, sb, S_ROWS, send_s, recv_s, convert_s)
+
+    xs = (0, 1, 3, 2)
+    zp, zm = near[0], near[1]
+    xp, xm = near[2], near[3]
+
+    def f1_own(t):
+        for to in (xp, xm, near[4], zp, zm, partner):
+            t.put(dev, to, own=True)
+        t.convert(t.own, 0, dev * t.rows)
+
+    def f1_x(t, j):
+        d = at(0, xs[j], 0)
+        t.wait(d)
+        for to in (zp, zm, partner):
+            t.put(d, to)
+        t.take(d)
+
+    def f1_z(t, k, j, s):
+        d = at(-k if s == 0 else k, xs[j], 0)
+        t.wait(d)
+        t.put(d, zp if s == 0 else zm, half=s if k == 3 else None)
+        t.put(d, partner)
+        t.take(d)
+
+    def f1_last(t, j):
+        d = at(4, xs[j], 0)
+        t.wait(d, 0)
+        t.wait(d, 1)
+        t.put(d, partner)
+        t.take(d)
+
+    zs = (0, -1, 1, -2, 2, -3, 3, 4)
+
+    def f2_own(t):
+        for to in (zp, zm, xp, xm, partner):
+            t.put(dev, to, own=True)
+        t.convert(t.own, 0, dev * t.rows)
+
+    def f2_z(t, m):
+        d = at(zs[m], 0, 1)
+        if m == 7:
+            t.wait(d, 0)
+            t.wait(d, 1)
+        else:
+            t.wait(d)
+            s = (m + 1) % 2
+            t.put(d, zp if s == 0 else zm, half=s if m >= 5 else None)
+        for to in (xp, xm, partner):
+            t.put(d, to)
+        t.take(d)
+
+    def f2_x(t, m, s):
+        d = at(zs[m], 3 if s == 0 else 1, 1)
+        t.wait(d)
+        t.put(d, xp if s == 0 else xm, half=s)
+        t.put(d, partner)
+        t.take(d)
+
+    def f2_x2(t, m):
+        d = at(zs[m], 2, 1)
+        t.wait(d, 0)
+        t.wait(d, 1)
+        t.put(d, partner)
+        t.take(d)
+
+    def part(f, *a):
+        return functools.partial(f, *a)
+
+    def f1_zs(t, k):
+        return [part(f1_z, t, k, j, s) for j in range(4) for s in range(2)]
+
+    def f2_xs(t, m):
+        return [part(f2_x, t, m, 0), part(f2_x, t, m, 1)]
+
+    x_all = lambda t: [part(f1_x, t, j) for j in (1, 2, 3)]
+    early0 = (
+        [part(f1_own, st), part(f1_own, ut)]
+        + x_all(st) + f1_zs(st, 1) + x_all(ut) + f1_zs(st, 2) + f1_zs(ut, 1) + f1_zs(st, 3)
+        + [part(f1_last, st, j) for j in range(4)]
+    )
+    late0 = f1_zs(ut, 2) + f1_zs(ut, 3) + [part(f1_last, ut, j) for j in range(4)]
+
+    fz = lambda t, *ms: [part(f2_z, t, m) for m in ms]
+    fx = lambda t, *ms: sum([f2_xs(t, m) for m in ms], [])
+    f2 = lambda t, *ms: [part(f2_x2, t, m) for m in ms]
+    early1 = (
+        [part(f2_own, st), part(f2_own, ut)]
+        + fz(st, 1, 2) + fx(st, 0) + fz(st, 3, 4) + fz(ut, 1, 2) + fx(st, 1, 2) + f2(st, 0)
+        + fz(st, 5, 6) + fx(st, 3, 4) + f2(st, 1, 2) + fz(st, 7) + fx(ut, 0) + fz(ut, 3, 4)
+        + fx(st, 5, 6) + f2(st, 3, 4) + fx(st, 7) + f2(st, 5, 6, 7)
+    )
+    late1 = (
+        fx(ut, 1, 2) + fz(ut, 5, 6) + f2(ut, 0) + fx(ut, 3, 4) + fz(ut, 7) + f2(ut, 1, 2)
+        + fx(ut, 5, 6) + f2(ut, 3, 4) + fx(ut, 7) + f2(ut, 5, 6, 7)
+    )
+
+    order0 = [(0, xs[j]) for j in range(4)]
+    order0 += [((-k, k)[s], xs[j]) for k in (1, 2, 3) for j in range(4) for s in range(2)]
+    order0 += [(4, xs[j]) for j in range(4)]
+    order1 = [(0, 0)]
+
+    def walk(events):
+        out = []
+        for e in events:
+            f, a = e.func, e.args
+            if a[0] is not ut:
+                continue
+            if f is f2_z:
+                out.append((zs[a[1]], 0))
+            elif f is f2_x:
+                out.append((zs[a[1]], 3 if a[2] == 0 else 1))
+            elif f is f2_x2:
+                out.append((zs[a[1]], 2))
+        return out
+
+    order1 += walk(early1) + walk(late1)
+
+    def from_partner(t, i, c):
+        dz, dx = (order1, order0)[c][i]
+        d = at(dz, dx, 1 - c)
+        t.wait(d)
+        t.take(d)
+
+    for c, events in ((0, early0), (1, early1)):
+
+        @pl.when(core == c)
+        def _():
+            for e in events:
+                e()
+
+    @pl.loop(0, 32)
+    def _(i):
+        d = i * 2 + 1 - core
+        st.wait(d)
+        st.take(d)
+
+    for c in local_copies:
+        c.wait()
+    ks = [kc_s[j] for j in range(8)]
+
+    def phase1(t):
+        for n in range(NZ):
+            idx = srow_s.at[pl.ds(pl.multiple_of(t * NZ + n // 8 * 8, 8), 8)]
+            g[n : n + 1, :] = stab[pl.ds(idx[ks[n % 8]], 1), :]
+        a = jnp.broadcast_to(v0_ref[pl.ds(t, 1), :], (128, 128))
+        b = jnp.broadcast_to(v1_ref[pl.ds(t, 1), :], (128, 128))
+        m = jnp.where(sublane < 64, a, b).T
+        sv[pl.ds(pl.multiple_of(t * NZ, 128), 128), :] = g[...] * m
+
+    def phase2(t):
+        accs = [jnp.zeros((1, 128), jnp.float32) for _ in range(4)]
+        for n in range(NZ):
+            idx = urow_s.at[pl.ds(pl.multiple_of(t * NZ + n // 8 * 8, 8), 8)]
+            row = utab[pl.ds(idx[ks[n % 8]], 1), :]
+            accs[n % 4] = accs[n % 4] + row * sv[pl.ds(t * NZ + n, 1), :]
+        out_ref[pl.ds(t, 1), :] = (accs[0] + accs[1]) + (accs[2] + accs[3])
+
+    @pl.loop(0, STEPS)
+    def _(i):
+        for c, events in ((0, late0), (1, late1)):
+
+            @pl.when(core == c)
+            def _():
+                for e, event in enumerate(events):
+                    pl.when(i == e * STEPS // len(events))(event)
+                for e in range(32):
+                    pl.when(i == e)(part(from_partner, ut, e, c))
+
+        @pl.loop(0, TILES_STEP)
+        def _(j):
+            phase1(i * TILES_STEP + j)
+
+    @pl.loop(0, NT)
+    def _(t):
+        phase2(t)
+
+    st.sent()
+    ut.sent()
+
+
+def tile_sums(user_factor, sub_factor, nz_user, nz_sub, nz_value):
+    f32, i32, bf16 = jnp.float32, jnp.int32, jnp.bfloat16
+    u_in = jnp.concatenate([user_factor[:, :U_ROWS], user_factor[:, U_ROWS:]], axis=0).T
+    s_in = jnp.concatenate([sub_factor[:, :S_ROWS], sub_factor[:, S_ROWS:]], axis=0).T
+    urow = (nz_user // (2 * U_ROWS)) * U_ROWS + nz_user % U_ROWS
+    upper = (nz_user // U_ROWS) % 2 == 1
+    v0 = jnp.where(upper, 0.0, nz_value)
+    v1 = jnp.where(upper, nz_value, 0.0)
+    kc = jnp.arange(128, dtype=i32)
+    vmem = pl.BlockSpec(memory_space=pltpu.VMEM)
+    hbm = pl.BlockSpec(memory_space=pl.ANY)
+    acc = pl.pallas_call(
+        kernel,
+        out_shape=jax.ShapeDtypeStruct((NT, LANES), f32),
+        in_specs=[hbm, hbm, hbm, vmem, vmem, vmem, vmem],
+        out_specs=vmem,
+        scratch_shapes=[
+            pltpu.VMEM((DEVS * U_ROWS, LANES), bf16),
+            pltpu.VMEM((DEVS * S_ROWS, LANES), bf16),
+            pltpu.VMEM((DEVS * U_ROWS, LANES), f32),
+            pltpu.VMEM((DEVS * S_ROWS * 2, LANES), f32),
+            pltpu.VMEM((NT * NZ, LANES), f32),
+            pltpu.VMEM((NZ, LANES), f32),
+            pltpu.SMEM((128,), i32),
+            pltpu.SMEM((NT * NZ,), i32),
+            pltpu.SMEM((NT * NZ,), i32),
+            pltpu.SemaphoreType.DMA,
+            pltpu.SemaphoreType.DMA,
+            pltpu.SemaphoreType.DMA((DEVS, 2)),
+            pltpu.SemaphoreType.DMA((DEVS, 2)),
+            pltpu.SemaphoreType.DMA((3,)),
+        ],
+        compiler_params=pltpu.CompilerParams(
+            collective_id=0, has_side_effects=True, vmem_limit_bytes=58 * 2**20
+        ),
+    )(kc, urow.reshape(-1), nz_sub.reshape(-1), v0, v1, u_in, s_in)
+    return acc[:, :64] + acc[:, 64:]
 
 
 def cut_along(value, dim, peers):
@@ -29,36 +346,8 @@
     return joined_along(pieces, concats[1])
 
 
-def tile_sums(user_table, sub_table, nz_user, nz_sub, nz_value):
-    tile_count, tile_width = nz_user.shape
-    block_tiles = min(tile_count, 128)
-    block_count = tile_count // block_tiles
-
-    def one_block(block_args):
-        users_block, subs_block, vals_block = block_args
-        user_rows = jnp.take(user_table, users_block, axis=0).astype(jnp.float32)
-        sub_rows = jnp.take(sub_table, subs_block, axis=0).astype(jnp.float32)
-        return jnp.sum(user_rows * sub_rows * vals_block[:, :, None], axis=1)
-
-    block_sums = lax.map(
-        one_block,
-        (
-            nz_user.reshape(block_count, block_tiles, tile_width),
-            nz_sub.reshape(block_count, block_tiles, tile_width),
-            nz_value.reshape(block_count, block_tiles, tile_width),
-        ),
-    )
-    return block_sums.reshape(tile_count, block_sums.shape[2])
-
-
 def shards(nz_user, nz_sub, nz_value, tile_word, word_owner, user_factor, sub_factor):
-    users_all, subs_all = (
-        lax.all_gather(user_factor, "dev", axis=1, tiled=True),
-        lax.all_gather(sub_factor, "dev", axis=1, tiled=True),
-    )
-    user_table = jnp.transpose(users_all)
-    sub_table = jnp.transpose(subs_all)
-    tile_rows = tile_sums(user_table, sub_table, nz_user, nz_sub, nz_value)
+    tile_rows = tile_sums(user_factor, sub_factor, nz_user, nz_sub, nz_value)
     tile_count, rank_width = tile_rows.shape
     grp_size = lax.axis_size("grp")
     dev_size = lax.axis_size("dev")

time: 298 us -> 127 us (0.43)
  local copies, waits for them, and re-layouts: 129 us -> 7.11 us
  waiting for transfers between devices: 113 us -> 11.5 us
  Pallas kernels: 0 us -> 73.8 us
  between operations: 13.5 us -> 0.17 us
  other arithmetic: 15.4 us -> 3.66 us
    gather x2 -> x0, local copies, waits for them, and re-layouts: 121 us -> none  [the longest x1 63.3 us: one_block(): user_rows = jnp.take(user_table, users_block, axis=0).astype(jnp.float32)]
    all_gather x2 -> x0, waiting for transfers between devices: 102 us -> none  [the longest x1 60.6 us: shards(): lax.all_gather(sub_factor, 'dev', axis=1, tiled=True)]
    pallas_call x0 -> x1, Pallas kernels: none -> 73.8 us  [tile_sums(): pl.pallas_call(kernel, out_shape=jax.ShapeDtypeStruct((NT, LANES), f32),...]
    reduce_sum x1 -> x0, other arithmetic: 10.6 us -> none  [one_block(): return jnp.sum(user_rows * sub_rows * vals_block[:, :, None], axis=1)]
  transfers between devices with their start and end apart: 4 -> 2, of which waited for: 3 -> 1; matrix products, arithmetic and copies ran while one was open for 48% -> 6% of each run, Pallas kernels for 0% -> 59%
where the time goes in v1:
time: 127 us; the launch traced here: 126 us
  Pallas kernels  73.8 us (58%)
  starting transfers between devices  26.6 us (21%)
  waiting for transfers between devices  11.5 us (9%)
  local copies, waits for them, and re-layouts  7.11 us (6%)
  other arithmetic  3.66 us (3%)
  matrix products  3.34 us (3%)
    pallas_call x1, Pallas kernels, tile_sums(): pl.pallas_call(kernel, out_shape=jax.ShapeDtypeStruct((NT, LANES), f32),...  73.8 us
    all_to_all x2, starting transfers between devices, exchange_both(): lax.all_to_all(pieces, axis, split_axis=0, concat_axis=0, tiled=True)  26.6 us
    all_to_all x2, waiting for transfers between devices, exchange_both(): lax.all_to_all(pieces, axis, split_axis=0, concat_axis=0, tiled=True)  11.5 us
    unnamed x18, local copies, waits for them, and re-layouts  2.68 us
  transfers between devices with their start and end apart: 2, of which 1 were waited for; matrix products, arithmetic and copies ran while one was open for 6% of the time, Pallas kernels for 59%

profile of v1, /device:TPU:1, one launch (start us, length us, event | category | flops | bytes accessed | tf_op | source)
XLA Modules:
  0.0 126.2 jit_solution(12130767848548231515)
XLA Ops:
  0.0 0.7 copy-done.6
  0.7 0.1 copy-done
  0.8 1.1 gather_fusion
  2.0 0.3 fusion
  2.4 0.1 convert_reduce_fusion
  2.5 0.3 fusion.1
  2.8 0.1 reshape_reshape.14
  2.9 0.7 copy.67
  3.6 15.6 %all-to-all-start.1 = ((f32[256,1,1,2]{3,2,1,0:T(1,128)}), f32[256,1,1,2]{3,2,1,0:T(1,128)S(1)}, u32[]{:S(2)}, u32[]{:S(2)}) async-start(f32[256,1,1,2]{3,2,1,0:T(1,128)} %bitcast.12), calls=%async_computation.1 | async-start | bytes 262144 | tf_op jit(solution)/shard_map/all_to_all | solution.py:344
  19.3 0.1 copy.69
  19.5 0.1 copy.70
  19.6 0.6 copy-done.5
  20.2 0.1 copy.71
  20.3 0.1 copy.72
  20.5 0.6 copy-done.2
  21.1 0.7 fusion.11.urow_ref
  21.7 0.2 copy-done.3
  21.9 0.7 broadcast_select_fusion
  22.6 0.6 broadcast_select_fusion.1.v0_ref
  23.2 0.8 maximum_bitcast_fusion.u_in
  24.0 0.7 maximum_bitcast_fusion.1.s_in
  24.7 0.5 iota.23.kc_ref
  25.2 73.8 %shard_map.73 = f32[128,128]{1,0:T(8,128)} custom-call(s32[128]{0:T(128)} %iota.23.kc_ref, s32[16384]{0:T(1024)} %fusion.11.urow_ref, s32[16384]{0:T(1024)} %bitcast.38, f32[128,128]{1,0:T(8,128)} %broadcast_select_fusion.1.v0_ref, f32[128,128]{1,0:T(8,128)} %get-tuple-element.8.v1_ref, bf16[512,128]{1,0:T(8,128)(2,1)} %maximum_bitcast_fusion.u_in, ...), custom_call_target="tpu_custom_call" | custom-call | tf_op jit(solution)/shard_map/pallas_call | solution.py:298
  99.1 1.4 %fusion.2 = f32[512,64]{1,0:T(8,128)S(1)} fusion(s32[128]{0:T(128)S(1)} %get-tuple-element.14, f32[128,128]{1,0:T(8,128)} %shard_map.73), kind=kOutput, calls=%fused_computation.8 | convolution fusion | flops 50405376 | bytes 262656 | tf_op jit(solution)/shard_map/ts,tr->sr/dot_general | solution.py:378
  100.6 0.8 copy.59
  101.3 11.0 %all-to-all-start = ((f32[256,1,1,128]{3,2,1,0:T(1,128)}), f32[256,1,1,128]{3,2,1,0:T(1,128)S(1)}, u32[]{:S(2)}, u32[]{:S(2)}) async-start(f32[256,1,1,128]{3,2,1,0:T(1,128)} %bitcast.6), calls=%async_computation | async-start | bytes 262144 | tf_op jit(solution)/shard_map/all_to_all | solution.py:344
  112.3 0.3 fusion.17
  112.7 0.1 convert_element_type.35
  112.8 0.6 copy.65
  113.4 0.2 convert_element_type.37
  113.5 11.5 %all-to-all-done = f32[256,1,1,128]{3,2,1,0:T(1,128)S(1)} async-done(((f32[256,1,1,128]{3,2,1,0:T(1,128)}), f32[256,1,1,128]{3,2,1,0:T(1,128)S(1)}, u32[]{:S(2)}, u32[]{:S(2)}) %all-to-all-start) | async-done | bytes 131104 | tf_op jit(solution)/shard_map/all_to_all | solution.py:344
  125.2 1.1 convolution_add_fusion
  (22 shorter events, 0.4 us)
Async XLA Ops:
  0.0 0.8 copy-start
  0.0 0.7 copy-start.6
  3.6 15.7 %copy-start.4 = (bf16[64,1024]{1,0:T(8,128)(2,1)S(1)}, bf16[64,1024]{1,0:T(8,128)(2,1)}, u32[]{:S(2)}) copy-start(bf16[64,1024]{1,0:T(8,128)(2,1)} %param.12) | copy-start | bytes 393220
  3.6 97.7 %all-to-all-start.1 = ((f32[256,1,1,2]{3,2,1,0:T(1,128)}), f32[256,1,1,2]{3,2,1,0:T(1,128)S(1)}, u32[]{:S(2)}, u32[]{:S(2)}) async-start(f32[256,1,1,2]{3,2,1,0:T(1,128)} %bitcast.12), calls=%async_computation.1 | async-start | bytes 262144 | tf_op jit(solution)/shard_map/all_to_all | solution.py:344
  19.4 0.8 copy-start.5
  20.2 0.8 copy-start.2
  21.1 0.8 copy-start.3
  101.3 11.0 %copy-start.1 = (f32[128,128]{1,0:T(8,128)S(1)}, f32[128,128]{1,0:T(8,128)}, u32[]{:S(2)}) copy-start(f32[128,128]{1,0:T(8,128)} %shard_map.73) | copy-start | bytes 196612
  101.3 23.7 %all-to-all-start = ((f32[256,1,1,128]{3,2,1,0:T(1,128)}), f32[256,1,1,128]{3,2,1,0:T(1,128)S(1)}, u32[]{:S(2)}, u32[]{:S(2)}) async-start(f32[256,1,1,128]{3,2,1,0:T(1,128)} %bitcast.6), calls=%async_computation | async-start | bytes 262144 | tf_op jit(solution)/shard_map/all_to_all | solution.py:344

commit v2 on v1

--- a/solution.py
+++ b/solution.py
@@ -17,9 +17,11 @@
 
 
 def kernel(
-    kc_ref, urow_ref, srow_ref, v0_ref, v1_ref, u_in, s_in, out_ref,
-    ub, sb, utab, stab, sv, g, kc_s, urow_s, srow_s,
-    send_u, send_s, recv_u, recv_s, loc,
+    kc_ref, word_ref, owner_ref, srow_ref, user_ref, value_ref, uf_ref, sf_ref, out_ref,
+    ub, sb, utab, stab, sv, g, u_in, s_in, urow_v, v0_ref, v1_ref, sums,
+    id_out, id_mid, id_turn, id_in, row_out, row_mid, row_turn, row_in, slots,
+    kc_s, word_s, owner_s, urow_s, srow_s,
+    send_u, send_s, recv_u, recv_s, loc, send_x, recv_x,
 ):
     grp = lax.axis_index("grp")
     dev = lax.axis_index("dev")
@@ -31,12 +33,29 @@
     def at(dz, dx, c):
         return ((z + dz + 8) % 8) * 8 + ((x + dx + 4) % 4) * 2 + c
 
-    local_copies = [
-        pltpu.make_async_copy(a, b, loc.at[i])
-        for i, (a, b) in enumerate(((kc_ref, kc_s), (srow_ref, srow_s), (urow_ref, urow_s)))
-    ]
+    me = grp * DEVS + dev
+    quad = grp * 8 + dev % 8
+
+    def in_plane(q):
+        return (q // 8, z * 8 + q % 8)
+
+    pairs = ((word_ref, word_s), (owner_ref, owner_s), (kc_ref, kc_s), (srow_ref, srow_s))
+    local_copies = [pltpu.make_async_copy(a, b, loc.at[i]) for i, (a, b) in enumerate(pairs)]
     for c in local_copies:
         c.start()
+
+    for src, dst, rows in ((uf_ref, u_in, U_ROWS), (sf_ref, s_in, S_ROWS)):
+        for i in range(rows // 128):
+            a = src[:, i * 128 : (i + 1) * 128].astype(jnp.float32)
+            b = src[:, rows + i * 128 : rows + (i + 1) * 128].astype(jnp.float32)
+            t = jnp.concatenate([a, b], axis=0).T
+            dst[i * 128 : (i + 1) * 128, :] = t.astype(jnp.bfloat16)
+
+    users = user_ref[...]
+    urow_v[...] = (users // (2 * U_ROWS)) * U_ROWS + users % U_ROWS
+    upper = (users // U_ROWS) % 2 == 1
+    v0_ref[...] = jnp.where(upper, 0.0, value_ref[...])
+    v1_ref[...] = jnp.where(upper, value_ref[...], 0.0)
 
     barrier = pltpu.get_barrier_semaphore()
     near = [
@@ -47,9 +66,17 @@
         at(0, 2, core),
         partner,
     ]
-    for n in near:
-        pl.semaphore_signal(barrier, inc=1, device_id=(grp, n), device_id_type=MESH)
-    pl.semaphore_wait(barrier, len(near))
+    for i in range(1, 8):
+        to = ((z + i) % 8) * 8 + dev % 8
+        pl.semaphore_signal(barrier, inc=1, device_id=(grp, to), device_id_type=MESH)
+    for i in range(1, 32):
+        to = in_plane((quad + i) % 32)
+        pl.semaphore_signal(barrier, inc=1, device_id=to, device_id_type=MESH)
+    pl.semaphore_wait(barrier, 38)
+
+    copy_u = pltpu.make_async_copy(urow_v, urow_s, loc.at[4])
+    copy_u.start()
+    local_copies.append(copy_u)
 
     class Table:
         def __init__(self, own, buf, rows, send, recv, convert):
@@ -227,12 +254,98 @@
         t.wait(d)
         t.take(d)
 
+    def x_copy(src, dst, way, to):
+        return pltpu.make_async_remote_copy(
+            src_ref=src, dst_ref=dst, send_sem=send_x.at[way], recv_sem=recv_x.at[way],
+            device_id=to, device_id_type=MESH,
+        )
+
+    def x_first(out, mid, way):
+        for i in range(1, 8):
+            zt = (z + i) % 8
+            src = out.at[pl.ds(pl.multiple_of(zt * 32, 32), 32), :]
+            dst = mid.at[pl.ds(pl.multiple_of(z * 40, 8), 32), :]
+            x_copy(src, dst, way, (grp, zt * 8 + dev % 8)).start()
+        mid[pl.ds(pl.multiple_of(z * 40, 8), 32), :] = out[pl.ds(pl.multiple_of(z * 32, 32), 32), :]
+
+    def x_wait(buf, rows, way):
+        ref = buf.at[pl.ds(0, rows), :]
+        x_copy(ref, ref, way, (grp, partner)).wait_recv()
+
+    def x_second(mid, turn, into, way):
+        x_wait(mid, 224, way)
+        for q in range(32):
+            turn[q * 8 : q * 8 + 8, :] = mid[pl.ds(q, 8, stride=40), :]
+        for i in range(1, 32):
+            q = (quad + i) % 32
+            src = turn.at[pl.ds(pl.multiple_of(q * 8, 8), 8), :]
+            dst = into.at[pl.ds(pl.multiple_of(quad * 8, 8), 8), :]
+            x_copy(src, dst, way + 1, in_plane(q)).start()
+        own = pl.ds(pl.multiple_of(quad * 8, 8), 8)
+        into[own, :] = turn[own, :]
+
+    def x_sent(buf, way):
+        for w, rows in ((way, 224), (way + 1, 248)):
+            ref = buf.at[pl.ds(0, rows), :]
+            x_copy(ref, ref, w, (grp, partner)).wait_send()
+
+    def routing():
+        local_copies[0].wait()
+        local_copies[1].wait()
+        lane1 = lax.broadcasted_iota(jnp.int32, (1, 128), 1)
+
+        def look(i, row):
+            for j in range(8):
+                t = i * 8 + j
+                row = jnp.where(lane1 == t, owner_s[word_s[t]], row)
+            return row
+
+        row = lax.fori_loop(0, NT // 8, look, jnp.zeros((1, 128), jnp.int32))
+        across = jnp.broadcast_to(row, (128, 128))
+        down = across.T
+        same = (down // 64 == across // 64) & (sublane < lane)
+        place = jnp.sum(same.astype(jnp.float32), axis=0, keepdims=True)
+        owner = row // 64
+        to = (owner // 8) % 8 * 32 + owner // 64 * 8 + owner % 8
+        dest = lax.broadcasted_iota(jnp.int32, (256, 128), 0)
+        far = owner != me
+        ids = (down % 64 + 1).astype(jnp.bfloat16)
+        found = []
+        for p in range(CAP):
+            hit = (to == dest) & far & (place == p)
+            table = hit.astype(jnp.float32).astype(jnp.bfloat16)
+            slots[p * 256 : (p + 1) * 256, :] = table
+            found.append(jnp.dot(table, ids, preferred_element_type=jnp.float32))
+        lane_w = lax.broadcasted_iota(jnp.int32, (256, 128), 1)
+        id_out[...] = jnp.where(lane_w < 64, found[0], found[1]) - 1.0
+        own = (down // 64 == me) & (down % 64 == lane)
+        slots[512:640, :] = own.astype(jnp.float32).astype(jnp.bfloat16)
+
+    def thirds(v):
+        hi = v.astype(jnp.bfloat16)
+        rest = v - hi.astype(jnp.float32)
+        mid = rest.astype(jnp.bfloat16)
+        low = (rest - mid.astype(jnp.float32)).astype(jnp.bfloat16)
+        return hi, mid, low
+
     for c, events in ((0, early0), (1, early1)):
 
         @pl.when(core == c)
         def _():
-            for e in events:
+            for e in events[:2]:
                 e()
+
+    routing()
+    x_first(id_out, id_mid, 0)
+
+    for c, events in ((0, early0), (1, early1)):
+
+        @pl.when(core == c)
+        def _():
+            for e in events[2:]:
+                e()
+
+    x_second(id_mid, id_turn, id_in, 0)
 
     @pl.loop(0, 32)
     def _(i):
@@ -240,14 +353,14 @@
         st.wait(d)
         st.take(d)
 
-    for c in local_copies:
+    for c in local_copies[2:]:
         c.wait()
     ks = [kc_s[j] for j in range(8)]
 
     def phase1(t):
         for n in range(NZ):
-            idx = srow_s.at[pl.ds(pl.multiple_of(t * NZ + n // 8 * 8, 8), 8)]
-            g[n : n + 1, :] = stab[pl.ds(idx[ks[n % 8]], 1), :]
+            idx = srow_s.at[pl.ds(t, 1), pl.ds(n // 8 * 8, 8)]
+            g[n : n + 1, :] = stab[pl.ds(idx[0, ks[n % 8]], 1), :]
         a = jnp.broadcast_to(v0_ref[pl.ds(t, 1), :], (128, 128))
         b = jnp.broadcast_to(v1_ref[pl.ds(t, 1), :], (128, 128))
         m = jnp.where(sublane < 64, a, b).T
@@ -256,10 +369,10 @@
     def phase2(t):
         accs = [jnp.zeros((1, 128), jnp.float32) for _ in range(4)]
         for n in range(NZ):
-            idx = urow_s.at[pl.ds(pl.multiple_of(t * NZ + n // 8 * 8, 8), 8)]
-            row = utab[pl.ds(idx[ks[n % 8]], 1), :]
+            idx = urow_s.at[pl.ds(t, 1), pl.ds(n // 8 * 8, 8)]
+            row = utab[pl.ds(idx[0, ks[n % 8]], 1), :]
             accs[n % 4] = accs[n % 4] + row * sv[pl.ds(t * NZ + n, 1), :]
-        out_ref[pl.ds(t, 1), :] = (accs[0] + accs[1]) + (accs[2] + accs[3])
+        sums[pl.ds(t, 1), :] = (accs[0] + accs[1]) + (accs[2] + accs[3])
 
     @pl.loop(0, STEPS)
     def _(i):
@@ -280,25 +393,48 @@
     def _(t):
         phase2(t)
 
+    total = sums[...]
+    total = total + pltpu.roll(total, 64, 1)
+    parts = thirds(total)
+    lane_w = lax.broadcasted_iota(jnp.int32, (256, 128), 1)
+    picked = []
+    for p in range(CAP):
+        table = slots[p * 256 : (p + 1) * 256, :]
+        hi, mid, low = (jnp.dot(table, v, preferred_element_type=jnp.float32) for v in parts)
+        picked.append((hi + mid) + low)
+    row_out[...] = jnp.where(lane_w < 64, picked[0], picked[1])
+    x_first(row_out, row_mid, 2)
+
+    def collect(table, v):
+        hi, mid, low = (
+            lax.dot_general(w, table, (((0,), (0,)), ((), ())), preferred_element_type=jnp.float32)
+            for w in thirds(v)
+        )
+        return (hi + mid) + low
+
+    own_part = collect(slots[512:640, :], total)
+    x_wait(id_in, 248, 1)
+    hits = (id_in[...] == (lane_w % 64).astype(jnp.float32)).astype(jnp.float32).astype(jnp.bfloat16)
     st.sent()
     ut.sent()
-
-
-def tile_sums(user_factor, sub_factor, nz_user, nz_sub, nz_value):
+    x_sent(id_out, 0)
+    x_second(row_mid, row_turn, row_in, 2)
+    x_wait(row_in, 248, 3)
+    far_part = collect(hits, row_in[...])
+    out_ref[...] = (own_part[:64, :64] + far_part[:64, :64]) + far_part[64:, 64:]
+    x_sent(row_out, 2)
+
+
+def shards(nz_user, nz_sub, nz_value, tile_word, word_owner, user_factor, sub_factor):
     f32, i32, bf16 = jnp.float32, jnp.int32, jnp.bfloat16
-    u_in = jnp.concatenate([user_factor[:, :U_ROWS], user_factor[:, U_ROWS:]], axis=0).T
-    s_in = jnp.concatenate([sub_factor[:, :S_ROWS], sub_factor[:, S_ROWS:]], axis=0).T
-    urow = (nz_user // (2 * U_ROWS)) * U_ROWS + nz_user % U_ROWS
-    upper = (nz_user // U_ROWS) % 2 == 1
-    v0 = jnp.where(upper, 0.0, nz_value)
-    v1 = jnp.where(upper, nz_value, 0.0)
     kc = jnp.arange(128, dtype=i32)
     vmem = pl.BlockSpec(memory_space=pltpu.VMEM)
     hbm = pl.BlockSpec(memory_space=pl.ANY)
-    acc = pl.pallas_call(
+    rows = pltpu.VMEM((256, LANES), f32)
+    return pl.pallas_call(
         kernel,
-        out_shape=jax.ShapeDtypeStruct((NT, LANES), f32),
-        in_specs=[hbm, hbm, hbm, vmem, vmem, vmem, vmem],
+        out_shape=jax.ShapeDtypeStruct((64, 64), f32),
+        in_specs=[hbm, hbm, hbm, hbm, vmem, vmem, vmem, vmem],
         out_specs=vmem,
         scratch_shapes=[
             pltpu.VMEM((DEVS * U_ROWS, LANES), bf16),
@@ -307,97 +443,32 @@
             pltpu.VMEM((DEVS * S_ROWS * 2, LANES), f32),
             pltpu.VMEM((NT * NZ, LANES), f32),
             pltpu.VMEM((NZ, LANES), f32),
+            pltpu.VMEM((U_ROWS, LANES), bf16),
+            pltpu.VMEM((S_ROWS, LANES), bf16),
+            pltpu.VMEM((NT, NZ), i32),
+            pltpu.VMEM((NT, NZ), f32),
+            pltpu.VMEM((NT, NZ), f32),
+            pltpu.VMEM((NT, LANES), f32),
+            rows, pltpu.VMEM((320, LANES), f32), rows, rows,
+            rows, pltpu.VMEM((320, LANES), f32), rows, rows,
+            pltpu.VMEM((640, LANES), bf16),
             pltpu.SMEM((128,), i32),
-            pltpu.SMEM((NT * NZ,), i32),
-            pltpu.SMEM((NT * NZ,), i32),
+            pltpu.SMEM((NT,), i32),
+            pltpu.SMEM((16384,), i32),
+            pltpu.SMEM((NT, NZ), i32),
+            pltpu.SMEM((NT, NZ), i32),
             pltpu.SemaphoreType.DMA,
             pltpu.SemaphoreType.DMA,
             pltpu.SemaphoreType.DMA((DEVS, 2)),
             pltpu.SemaphoreType.DMA((DEVS, 2)),
-            pltpu.SemaphoreType.DMA((3,)),
+            pltpu.SemaphoreType.DMA((5,)),
+            pltpu.SemaphoreType.DMA((4,)),
+            pltpu.SemaphoreType.DMA((4,)),
         ],
         compiler_params=pltpu.CompilerParams(
             collective_id=0, has_side_effects=True, vmem_limit_bytes=58 * 2**20
         ),
-    )(kc, urow.reshape(-1), nz_sub.reshape(-1), v0, v1, u_in, s_in)
-    return acc[:, :64] + acc[:, 64:]
-
-
-def cut_along(value, dim, peers):
-    shape = value.shape
-    pieces = value.reshape(*shape[:dim], peers, shape[dim] // peers, *shape[dim + 1 :])
-    return jnp.moveaxis(pieces, dim, 0)
-
-
-def joined_along(pieces, dim):
-    pieces = jnp.moveaxis(pieces, 0, dim)
-    shape = pieces.shape
-    return pieces.reshape(*shape[:dim], shape[dim] * shape[dim + 1], *shape[dim + 2 :])
-
-
-def exchange_both(value, axis, axes, splits, concats):
-    sizes = [lax.axis_size(a) for a in axes]
-    pieces = cut_along(value, splits[0], sizes[0])
-    pieces = jnp.moveaxis(cut_along(pieces, splits[1] + 1, sizes[1]), 0, 1)
-    inside = pieces.shape[2:]
-    pieces = pieces.reshape(-1, *inside)
-    pieces = lax.all_to_all(pieces, axis, split_axis=0, concat_axis=0, tiled=True)
-    pieces = joined_along(pieces.reshape(*sizes, *inside), concats[0] + 1)
-    return joined_along(pieces, concats[1])
-
-
-def shards(nz_user, nz_sub, nz_value, tile_word, word_owner, user_factor, sub_factor):
-    tile_rows = tile_sums(user_factor, sub_factor, nz_user, nz_sub, nz_value)
-    tile_count, rank_width = tile_rows.shape
-    grp_size = lax.axis_size("grp")
-    dev_size = lax.axis_size("dev")
-    devices_all = grp_size * dev_size
-    words_total = word_owner.shape[0]
-    words_local = words_total // devices_all
-    out_rows = jnp.take(word_owner, tile_word)
-    self_index = lax.axis_index("grp") * dev_size + lax.axis_index("dev")
-    owner_dev = out_rows // words_local
-    local_row = out_rows - owner_dev * words_local
-    owned = owner_dev == self_index
-    columns = jnp.arange(words_local, dtype=jnp.int32)
-    own_table = (owned[:, None] & (local_row[:, None] == columns[None, :])).astype(jnp.float32)
-    own_part = jnp.einsum("tr,tk->rk", tile_rows, own_table, precision=lax.Precision.HIGHEST)
-    peer_ids = jnp.arange(devices_all, dtype=jnp.int32)
-    outgoing = (jnp.logical_not(owned)[:, None] & (owner_dev[:, None] == peer_ids[None, :])).astype(
-        jnp.float32
-    )
-    tile_ids = jnp.arange(tile_count, dtype=jnp.int32)
-    earlier_table = (tile_ids[:, None] > tile_ids[None, :]).astype(jnp.float32)
-    earlier = jnp.dot(
-        earlier_table, outgoing, precision=lax.Precision.HIGHEST, preferred_element_type=jnp.float32
-    )
-    position = jnp.sum(earlier * outgoing, axis=1).astype(jnp.int32)
-    send_slot = jnp.where(owned, devices_all * CAP, owner_dev * CAP + position)
-    slot_ids = jnp.arange(devices_all * CAP, dtype=jnp.int32)
-    slot_table = (send_slot[:, None] == slot_ids[None, :]).astype(jnp.float32)
-    send_rows = jnp.einsum("ts,tr->sr", slot_table, tile_rows, precision=lax.Precision.HIGHEST)
-    filled = jnp.sum(slot_table, axis=0)
-    send_ids = (
-        jnp.dot(
-            local_row.astype(jnp.float32),
-            slot_table,
-            precision=lax.Precision.HIGHEST,
-            preferred_element_type=jnp.float32,
-        )
-        + filled
-        - 1.0
-    )
-    send_rows = send_rows.reshape(grp_size, dev_size, CAP * rank_width)
-    send_ids = send_ids.reshape(grp_size, dev_size, CAP)
-    got_rows, got_ids = (
-        exchange_both(send_rows, ("dev", "grp"), ("dev", "grp"), (1, 0), (1, 0)),
-        exchange_both(send_ids, ("dev", "grp"), ("dev", "grp"), (1, 0), (1, 0)),
-    )
-    got_rows = got_rows.reshape(devices_all * CAP, rank_width)
-    got_ids = got_ids.reshape(devices_all * CAP).astype(jnp.int32)
-    got_table = (got_ids[:, None] == columns[None, :]).astype(jnp.float32)
-    far_part = jnp.einsum("sr,sk->rk", got_rows, got_table, precision=lax.Precision.HIGHEST)
-    return own_part + far_part
+    )(kc, tile_word, word_owner, nz_sub, nz_user, nz_value, user_factor, sub_factor)
 
 
 def solution(mesh):

time: 127 us -> 97 us (0.76)
  starting transfers between devices: 26.6 us -> 0 us
  Pallas kernels: 73.8 us -> 95 us
  waiting for transfers between devices: 11.5 us -> 0 us
  local copies, waits for them, and re-layouts: 7.11 us -> 1.89 us
  other arithmetic: 3.66 us -> 0 us
  matrix products: 3.34 us -> 0 us
    all_to_all x2 -> x0, starting transfers between devices: 26.6 us -> none  [exchange_both(): lax.all_to_all(pieces, axis, split_axis=0, concat_axis=0, tiled=True)]
    pallas_call x1, Pallas kernels: 73.8 us -> 95 us  [shards(): pl.pallas_call(kernel, out_shape=jax.ShapeDtypeStruct((64, 64), f32), in_...]
    all_to_all x2 -> x0, waiting for transfers between devices: 11.5 us -> none  [exchange_both(): lax.all_to_all(pieces, axis, split_axis=0, concat_axis=0, tiled=True)]
    dot_general x5 -> x0, matrix products: 3.34 us -> none  [the longest x1 1.37 us: shards(): jnp.einsum('ts,tr->sr', slot_table, tile_rows, precision=lax.Precision.HI...]
    transpose x2 -> x0, other arithmetic: 1.48 us -> none  [the longest x1 0.78 us: tile_sums(): jnp.concatenate([user_factor[:, :U_ROWS], user_factor[:, U_ROWS:]], axis=0)]
    select_n x4 -> x0, other arithmetic: 1.35 us -> none  [the longest x1 0.7 us: tile_sums(): v1 = jnp.where(upper, nz_value, 0.0)]
    unnamed x18 -> x1, local copies, waits for them, and re-layouts: 2.68 us -> 1.38 us
  transfers between devices with their start and end apart: 2 -> 0, of which waited for: 1 -> 0; matrix products, arithmetic and copies ran while one was open for 6% -> 0% of each run, Pallas kernels for 59% -> 0%
where the time goes in v2:
time: 97 us; the launch traced here: 96.9 us
  Pallas kernels  95 us (98%)
  local copies, waits for them, and re-layouts  1.89 us (2%)
    pallas_call x1, Pallas kernels, shards(): pl.pallas_call(kernel, out_shape=jax.ShapeDtypeStruct((64, 64), f32), in_...  95 us

profile of v2, /device:TPU:1, one launch (start us, length us, event | category | flops | bytes accessed | tf_op | source)
XLA Modules:
  0.0 96.9 jit_solution(2330105873136794329)
XLA Ops:
  0.0 0.5 iota.3.kc_ref
  0.5 95.0 %shard_map.73 = f32[64,64]{1,0:T(8,128)} custom-call(s32[128]{0:T(128)} %iota.3.kc_ref, s32[128]{0:T(128)} %word_ref.1, s32[16384]{0:T(1024)} %owner_ref.1, s32[128,128]{1,0:T(8,128)} %srow_ref.1, s32[128,128]{1,0:T(8,128)} %user_ref.1, f32[128,128]{1,0:T(8,128)} %value_ref.1, bf16[64,1024]{1,0:T(8,128)(2,1)} %uf_ref.1, bf16[64,256]{1,0:T(8,128)(2,1)} %sf_ref.1), custom_call_target="tpu_custom_call" | custom-call | tf_op jit(solution)/shard_map/pallas_call | solution.py:434
  95.5 1.4 %copy.9 = f32[64,64]{1,0:T(8,128)} copy(f32[64,64]{1,0:T(8,128)} %shard_map.73) | data formatting | bytes 32768

commit v3 on v2

v3 whole, which is shorter than its diff:
```python
import functools

import jax
import jax.numpy as jnp
from jax import lax
from jax.experimental import pallas as pl
from jax.experimental.pallas import tpu as pltpu
from jax.sharding import PartitionSpec as P

CAP = 2
MESH = pl.DeviceIdType.MESH
NT, NZ, LANES = 128, 128, 128
DEVS = 64
U_ROWS, S_ROWS = 512, 128
ROWS = U_ROWS + S_ROWS
SIDE = (288, 160)
LAG_Y, LAG_PARTNER = 6, 8
ORDER = (
    (("x", 0, 1), ("x", 0, 3), ("z", -1, 0), ("z", 1, 0), ("x", 0, 2), ("z", -1, 1), ("z", 1, 1), ("z", -1, 3))
    + (("z", 1, 3), ("z", -2, 0), ("z", 2, 0), ("z", -1, 2), ("z", 1, 2), ("z", -2, 1), ("z", 2, 1), ("z", -2, 3))
    + (("z", 2, 3), ("z", -3, 0), ("z", 3, 0), ("z", -2, 2), ("z", 2, 2), ("z", -3, 1), ("z", 3, 1), ("z", -3, 3))
    + (("z", 3, 3), ("end", 4, 0), ("z", -3, 2), ("z", 3, 2), ("end", 4, 1), ("end", 4, 3), ("end", 4, 2)),
    (("z", -1, 0), ("z", 1, 0), ("x", 0, 1), ("x", 0, 3), ("x", -1, 1), ("x", -1, 3), ("z", -2, 0), ("x", 1, 1))
    + (("z", 2, 0), ("x", 1, 3), ("end", 0, 2), ("end", -1, 2), ("x", -2, 1), ("x", -2, 3), ("z", -3, 0), ("x", 2, 3))
    + (("z", 3, 0), ("x", 2, 1), ("end", 1, 2), ("end", -2, 2), ("x", -3, 3), ("x", -3, 1), ("end", 4, 0), ("x", 3, 1))
    + (("end", 2, 2), ("x", 3, 3), ("end", -3, 2), ("x", 4, 3), ("x", 4, 1), ("end", 3, 2), ("end", 4, 2)),
)


def kernel(
    kc_ref, word_ref, owner_ref, srow_ref, user_ref, value_ref, uf_ref, sf_ref, out_ref,
    buf, utab, stab, sv, g, own_in, urow_v, v0_ref, v1_ref, sums,
    id_out, id_mid, id_turn, id_in, row_out, row_mid, row_turn, row_in, slots,
    kc_s, word_s, owner_s, urow_s, srow_s,
    send_t, recv_t, loc, send_x, recv_x,
):
    grp = lax.axis_index("grp")
    dev = lax.axis_index("dev")
    z, x, core = dev // 8, (dev // 2) % 4, dev % 2
    partner = dev + 1 - 2 * core
    lane = lax.broadcasted_iota(jnp.int32, (128, 128), 1)
    sublane = lax.broadcasted_iota(jnp.int32, (128, 128), 0)

    def at(dz, dx, c):
        return ((z + dz + 8) % 8) * 8 + ((x + dx + 4) % 4) * 2 + c

    me = grp * DEVS + dev
    quad = grp * 8 + dev % 8

    def in_plane(q):
        return (q // 8, z * 8 + q % 8)

    pairs = ((word_ref, word_s), (owner_ref, owner_s), (kc_ref, kc_s), (srow_ref, srow_s))
    local_copies = [pltpu.make_async_copy(a, b, loc.at[i]) for i, (a, b) in enumerate(pairs)]
    for c in local_copies:
        c.start()

    for src, first, rows in ((uf_ref, 0, U_ROWS), (sf_ref, U_ROWS, S_ROWS)):
        for i in range(rows // 128):
            a = src[:, i * 128 : (i + 1) * 128].astype(jnp.float32)
            b = src[:, rows + i * 128 : rows + (i + 1) * 128].astype(jnp.float32)
            t = jnp.concatenate([a, b], axis=0).T
            own_in[first + i * 128 : first + (i + 1) * 128, :] = t.astype(jnp.bfloat16)

    users = user_ref[...]
    urow_v[...] = (users // (2 * U_ROWS)) * U_ROWS + users % U_ROWS
    upper = (users // U_ROWS) % 2 == 1
    v0_ref[...] = jnp.where(upper, 0.0, value_ref[...])
    v1_ref[...] = jnp.where(upper, value_ref[...], 0.0)

    barrier = pltpu.get_barrier_semaphore()
    for i in range(1, 8):
        to = ((z + i) % 8) * 8 + dev % 8
        pl.semaphore_signal(barrier, inc=1, device_id=(grp, to), device_id_type=MESH)
    for i in range(1, 32):
        to = in_plane((quad + i) % 32)
        pl.semaphore_signal(barrier, inc=1, device_id=to, device_id_type=MESH)
    pl.semaphore_wait(barrier, 38)

    copy_u = pltpu.make_async_copy(urow_v, urow_s, loc.at[4])
    copy_u.start()
    local_copies.append(copy_u)

    par = grp % 2
    y_up, y_down = (grp + 1) % 4, (grp + 3) % 4
    zp, zm, xp, xm = at(1, 0, core), at(-1, 0, core), at(0, 1, core), at(0, 3, core)
    x_far = at(0, 2, core)
    sent_rows = [0, 0]

    def shard(d, first, rows):
        return buf.at[pl.ds(pl.multiple_of(d * ROWS + first, 16), rows), :]

    def ring_rows(c, half=None):
        rows = ROWS - SIDE[c]
        first = par * SIDE[c]
        return (first, rows) if half is None else (first + half * (rows // 2), rows // 2)

    def copy(d, first, rows, sem, to, own=False):
        dst = shard(d, first, rows)
        src = own_in.at[pl.ds(pl.multiple_of(first, 16), rows), :] if own else dst
        return pltpu.make_async_remote_copy(
            src_ref=src, dst_ref=dst, send_sem=send_t, recv_sem=recv_t.at[d, sem],
            device_id=to, device_id_type=MESH,
        )

    def put(c, d, span, sem, to, own=False):
        copy(d, *span, sem, to, own).start()
        sent_rows[c] += span[1]

    def ring(c, d, to, half=None, own=False):
        put(c, d, ring_rows(c, half), 0 if half is None else half, (grp, to), own)

    def over(c, d):
        put(c, d, ring_rows(c), 0, (grp, partner))
        half = SIDE[c] // 2
        first = par * (ROWS - SIDE[c])
        put(c, d, (first, half), 2, (y_up, dev))
        put(c, d, (first + half, half), 3, (y_down, dev))

    def await_rows(d, span, sem):
        copy(d, *span, sem, (grp, partner)).wait_recv()

    def await_ring(c, d, half=None):
        await_rows(d, ring_rows(c, half), 0 if half is None else half)

    def take(src, base, d):
        @pl.loop(0, 4)
        def _(i):
            a = pl.multiple_of(base + i * 128, 128)
            b = pl.multiple_of(d * U_ROWS + i * 128, 128)
            utab[pl.ds(b, 128), :] = src[pl.ds(a, 128), :].astype(jnp.float32)

        v = src[pl.ds(pl.multiple_of(base + U_ROWS, 128), 128), :].astype(jnp.float32)
        r = pltpu.roll(v, 64, 1)
        a = pl.multiple_of(2 * d * S_ROWS, 128)
        stab[pl.ds(a, 128), :] = jnp.where(lane < 64, v, r)
        stab[pl.ds(a + 128, 128), :] = jnp.where(lane < 64, r, v)

    def own_shard(c):
        for to in (zp, zm, xp, xm) + ((x_far,) if c == 0 else ()):
            ring(c, dev, to, own=True)
        put(c, dev, (0, ROWS), 0, (grp, partner), own=True)

    def arrive(c, kind, dz, dx):
        d = at(dz, dx, c)
        if kind == "end":
            await_ring(c, d, 0)
            await_ring(c, d, 1)
        else:
            await_ring(c, d)
        if kind == "z":
            side = 0 if dz < 0 else 1
            ring(c, d, (zp, zm)[side], half=side if abs(dz) == 3 else None)
        if c == 0 and kind == "x":
            ring(c, d, zp)
            ring(c, d, zm)
        if c == 1 and dx == 0:
            ring(c, d, xp)
            ring(c, d, xm)
        if c == 1 and kind == "x":
            side = 0 if dx == 3 else 1
            ring(c, d, (xp, xm)[side], half=side)
        over(c, d)

    def arrive_y(c, dz, dx):
        d = at(dz, dx, c)
        half = SIDE[c] // 2
        first = (1 - par) * (ROWS - SIDE[c])
        await_rows(d, (first, half), 2)
        await_rows(d, (first + half, half), 3)
        put(c, d, (first, 2 * half), 2, (grp, partner))
        take(buf, d * ROWS, d)

    def arrive_partner(c, dz, dx):
        d = at(dz, dx, 1 - c)
        if dz == 0 and dx == 0:
            await_rows(d, (0, ROWS), 0)
        else:
            await_ring(1 - c, d)
            await_rows(d, ((1 - par) * (ROWS - SIDE[1 - c]), SIDE[1 - c]), 2)
        take(buf, d * ROWS, d)

    def masks(t):
        a = jnp.broadcast_to(v0_ref[pl.ds(t, 1), :], (128, 128))
        b = jnp.broadcast_to(v1_ref[pl.ds(t, 1), :], (128, 128))
        sv[pl.ds(pl.multiple_of(t * NZ, 128), 128), :] = jnp.where(sublane < 64, a, b).T

    def x_copy(src, dst, way, to):
        return pltpu.make_async_remote_copy(
            src_ref=src, dst_ref=dst, send_sem=send_x.at[way], recv_sem=recv_x.at[way],
            device_id=to, device_id_type=MESH,
        )

    def x_first(out, mid, way):
        for i in range(1, 8):
            zt = (z + i) % 8
            src = out.at[pl.ds(pl.multiple_of(zt * 32, 32), 32), :]
            dst = mid.at[pl.ds(pl.multiple_of(z * 40, 8), 32), :]
            x_copy(src, dst, way, (grp, zt * 8 + dev % 8)).start()
        mid[pl.ds(pl.multiple_of(z * 40, 8), 32), :] = out[pl.ds(pl.multiple_of(z * 32, 32), 32), :]

    def x_wait(buf, rows, way):
        ref = buf.at[pl.ds(0, rows), :]
        x_copy(ref, ref, way, (grp, partner)).wait_recv()

    def x_second(mid, turn, into, way):
        x_wait(mid, 224, way)
        for q in range(32):
            turn[q * 8 : q * 8 + 8, :] = mid[pl.ds(q, 8, stride=40), :]
        for i in range(1, 32):
            q = (quad + i) % 32
            src = turn.at[pl.ds(pl.multiple_of(q * 8, 8), 8), :]
            dst = into.at[pl.ds(pl.multiple_of(quad * 8, 8), 8), :]
            x_copy(src, dst, way + 1, in_plane(q)).start()
        own = pl.ds(pl.multiple_of(quad * 8, 8), 8)
        into[own, :] = turn[own, :]

    def x_sent(buf, way):
        for w, rows in ((way, 224), (way + 1, 248)):
            ref = buf.at[pl.ds(0, rows), :]
            x_copy(ref, ref, w, (grp, partner)).wait_send()

    def routing():
        local_copies[0].wait()
        local_copies[1].wait()
        lane1 = lax.broadcasted_iota(jnp.int32, (1, 128), 1)

        def look(i, row):
            for j in range(8):
                t = i * 8 + j
                row = jnp.where(lane1 == t, owner_s[word_s[t]], row)
            return row

        row = lax.fori_loop(0, NT // 8, look, jnp.zeros((1, 128), jnp.int32))
        across = jnp.broadcast_to(row, (128, 128))
        down = across.T
        same = (down // 64 == across // 64) & (sublane < lane)
        place = jnp.sum(same.astype(jnp.float32), axis=0, keepdims=True)
        owner = row // 64
        to = (owner // 8) % 8 * 32 + owner // 64 * 8 + owner % 8
        dest = lax.broadcasted_iota(jnp.int32, (256, 128), 0)
        far = owner != me
        ids = (down % 64 + 1).astype(jnp.bfloat16)
        found = []
        for p in range(CAP):
            hit = (to == dest) & far & (place == p)
            table = hit.astype(jnp.float32).astype(jnp.bfloat16)
            slots[p * 256 : (p + 1) * 256, :] = table
            found.append(jnp.dot(table, ids, preferred_element_type=jnp.float32))
        lane_w = lax.broadcasted_iota(jnp.int32, (256, 128), 1)
        id_out[...] = jnp.where(lane_w < 64, found[0], found[1]) - 1.0
        own = (down // 64 == me) & (down % 64 == lane)
        slots[512:640, :] = own.astype(jnp.float32).astype(jnp.bfloat16)

    def thirds(v):
        hi = v.astype(jnp.bfloat16)
        rest = v - hi.astype(jnp.float32)
        mid = rest.astype(jnp.bfloat16)
        low = (rest - mid.astype(jnp.float32)).astype(jnp.bfloat16)
        return hi, mid, low

    for c in (0, 1):
        pl.when(core == c)(functools.partial(own_shard, c))

    routing()
    x_first(id_out, id_mid, 0)
    take(own_in, 0, dev)

    def gather(c):
        mine = ORDER[c]
        theirs = (("", 0, 0),) + ORDER[1 - c]
        for i in range(31 + LAG_PARTNER + 1):
            if i < 31:
                arrive(c, *mine[i])

                @pl.loop(4 * i, 4 * i + 4)
                def _(t):
                    masks(t)

            if 0 <= i - LAG_Y < 31:
                arrive_y(c, *mine[i - LAG_Y][1:])
            if i - LAG_PARTNER >= 0:
                arrive_partner(c, *theirs[i - LAG_PARTNER][1:])

    for c in (0, 1):
        pl.when(core == c)(functools.partial(gather, c))
    assert sent_rows[0] == sent_rows[1] <= DEVS * ROWS

    x_second(id_mid, id_turn, id_in, 0)

    @pl.loop(124, NT)
    def _(t):
        masks(t)

    for c in local_copies[2:]:
        c.wait()
    ks = [kc_s[j] for j in range(8)]

    @pl.loop(0, NT)
    def _(t):
        def at_slot(index, n):
            return pl.ds(index.at[pl.ds(t, 1), pl.ds(n // 8 * 8, 8)][0, ks[n % 8]], 1)

        for n in range(NZ):
            g[n : n + 1, :] = stab[at_slot(srow_s, n), :]
        accs = [jnp.zeros((1, 128), jnp.float32) for _ in range(4)]
        for n in range(NZ):
            product = utab[at_slot(urow_s, n), :] * g[n : n + 1, :]
            accs[n % 4] = accs[n % 4] + product * sv[pl.ds(t * NZ + n, 1), :]
        sums[pl.ds(t, 1), :] = (accs[0] + accs[1]) + (accs[2] + accs[3])

    total = sums[...]
    total = total + pltpu.roll(total, 64, 1)
    parts = thirds(total)
    lane_w = lax.broadcasted_iota(jnp.int32, (256, 128), 1)
    picked = []
    for p in range(CAP):
        table = slots[p * 256 : (p + 1) * 256, :]
        hi, mid, low = (jnp.dot(table, v, preferred_element_type=jnp.float32) for v in parts)
        picked.append((hi + mid) + low)
    row_out[...] = jnp.where(lane_w < 64, picked[0], picked[1])
    x_first(row_out, row_mid, 2)

    def collect(table, v):
        hi, mid, low = (
            lax.dot_general(w, table, (((0,), (0,)), ((), ())), preferred_element_type=jnp.float32)
            for w in thirds(v)
        )
        return (hi + mid) + low

    own_part = collect(slots[512:640, :], total)
    x_wait(id_in, 248, 1)
    hits = (id_in[...] == (lane_w % 64).astype(jnp.float32)).astype(jnp.float32).astype(jnp.bfloat16)
    copy(0, 0, sent_rows[0], 0, (grp, partner)).wait_send()
    x_sent(id_out, 0)
    x_second(row_mid, row_turn, row_in, 2)
    x_wait(row_in, 248, 3)
    far_part = collect(hits, row_in[...])
    out_ref[...] = (own_part[:64, :64] + far_part[:64, :64]) + far_part[64:, 64:]
    x_sent(row_out, 2)


def shards(nz_user, nz_sub, nz_value, tile_word, word_owner, user_factor, sub_factor):
    f32, i32, bf16 = jnp.float32, jnp.int32, jnp.bfloat16
    kc = jnp.arange(128, dtype=i32)
    vmem = pl.BlockSpec(memory_space=pltpu.VMEM)
    hbm = pl.BlockSpec(memory_space=pl.ANY)
    rows = pltpu.VMEM((256, LANES), f32)
    return pl.pallas_call(
        kernel,
        out_shape=jax.ShapeDtypeStruct((64, 64), f32),
        in_specs=[hbm, hbm, hbm, hbm, vmem, vmem, vmem, vmem],
        out_specs=vmem,
        scratch_shapes=[
            pltpu.VMEM((DEVS * ROWS, LANES), bf16),
            pltpu.VMEM((DEVS * U_ROWS, LANES), f32),
            pltpu.VMEM((DEVS * S_ROWS * 2, LANES), f32),
            pltpu.VMEM((NT * NZ, LANES), f32),
            pltpu.VMEM((NZ, LANES), f32),
            pltpu.VMEM((ROWS, LANES), bf16),
            pltpu.VMEM((NT, NZ), i32),
            pltpu.VMEM((NT, NZ), f32),
            pltpu.VMEM((NT, NZ), f32),
            pltpu.VMEM((NT, LANES), f32),
            rows, pltpu.VMEM((320, LANES), f32), rows, rows,
            rows, pltpu.VMEM((320, LANES), f32), rows, rows,
            pltpu.VMEM((640, LANES), bf16),
            pltpu.SMEM((128,), i32),
            pltpu.SMEM((NT,), i32),
            pltpu.SMEM((16384,), i32),
            pltpu.SMEM((NT, NZ), i32),
            pltpu.SMEM((NT, NZ), i32),
            pltpu.SemaphoreType.DMA,
            pltpu.SemaphoreType.DMA((DEVS, 4)),
            pltpu.SemaphoreType.DMA((5,)),
            pltpu.SemaphoreType.DMA((4,)),
            pltpu.SemaphoreType.DMA((4,)),
        ],
        compiler_params=pltpu.CompilerParams(
            collective_id=0, has_side_effects=True, vmem_limit_bytes=58 * 2**20
        ),
    )(kc, tile_word, word_owner, nz_sub, nz_user, nz_value, user_factor, sub_factor)


def solution(mesh):
    return jax.shard_map(
        shards,
        mesh=mesh,
        in_specs=(
            P(("grp", "dev"), None),
            P(("grp", "dev"), None),
            P(("grp", "dev"), None),
            P(("grp", "dev")),
            P(),
            P(None, "dev"),
            P(None, "dev"),
        ),
        out_specs=P(None, ("grp", "dev")),
        check_vma=False,
    )
```

time: 97 us -> 83 us (0.86)
  Pallas kernels: 95 us -> 81 us
    pallas_call x1, Pallas kernels: 95 us -> 81 us  [shards(): pl.pallas_call(kernel, out_shape=jax.ShapeDtypeStruct((64, 64), f32), in_...]
where the time goes in v3:
time: 83 us; the launch traced here: 82.9 us
  Pallas kernels  81 us (98%)
  local copies, waits for them, and re-layouts  1.89 us (2%)
    pallas_call x1, Pallas kernels, shards(): pl.pallas_call(kernel, out_shape=jax.ShapeDtypeStruct((64, 64), f32), in_...  81 us

profile of v3, /device:TPU:1, one launch (start us, length us, event | category | flops | bytes accessed | tf_op | source)
XLA Modules:
  0.0 82.9 jit_solution(2013984973922931890)
XLA Ops:
  0.0 0.5 iota.3.kc_ref
  0.5 81.0 %shard_map.73 = f32[64,64]{1,0:T(8,128)} custom-call(s32[128]{0:T(128)} %iota.3.kc_ref, s32[128]{0:T(128)} %word_ref.1, s32[16384]{0:T(1024)} %owner_ref.1, s32[128,128]{1,0:T(8,128)} %srow_ref.1, s32[128,128]{1,0:T(8,128)} %user_ref.1, f32[128,128]{1,0:T(8,128)} %value_ref.1, bf16[64,1024]{1,0:T(8,128)(2,1)} %uf_ref.1, bf16[64,256]{1,0:T(8,128)(2,1)} %sf_ref.1), custom_call_target="tpu_custom_call" | custom-call | tf_op jit(solution)/shard_map/pallas_call | solution.py:349
  81.5 1.4 %copy.9 = f32[64,64]{1,0:T(8,128)} copy(f32[64,64]{1,0:T(8,128)} %shard_map.73) | data formatting | bytes 32768
